TPU v7x, 256 devices: a whole 4x4x8 slice. The times are simulated.
256 devices in a mesh: fsdp: 64 (over z, y, core), rep: 4 (over x).
Axes of the slice: x: 4, y: 4, z: 8, core: 2. Of those that a mesh axis runs over, the one named last changes fastest.
Arguments:
- partial_grad: bfloat16 [4, 64, 1024, 1024], P('rep', None, 'fsdp'), may hold values from -3 to 3
- owner_table: int32 [64, 2], replicated, may hold values from -1 to 63, as said below
- left_stat: float32 [64, 2, 1024, 1024], P('fsdp', None, None, 'rep'), may hold values from -6 to 6
- right_stat: float32 [64, 2, 1024, 1024], P('fsdp', None, None, 'rep'), may hold values from -6 to 6
- left_root: bfloat16 [64, 2, 1024, 1024], P('fsdp', None, None, 'rep'), may hold values from -0.1875 to 0.1875
- right_root: bfloat16 [64, 2, 1024, 1024], P('fsdp', None, None, 'rep'), may hold values from -0.1875 to 0.1875
Outputs:
- left_new: float32 [64, 2, 1024, 1024], P('fsdp', None, None, 'rep')
- right_new: float32 [64, 2, 1024, 1024], P('fsdp', None, None, 'rep')
- update: bfloat16 [64, 1024, 1024], P(None, 'fsdp', 'rep')
Inputs may be any that keep to these rules, and one draw needn't show every extreme that they name: `owner_table`: each of the 64 blocks stands in exactly one slot and -1 marks an empty slot; some owner fills all 2 slots and some owner has none.
All inputs are finite; a program needn't handle non-finite values.
Results may differ from a plain program's by a relative error of at most 0.014.
Values may be sent and summed in bfloat16 or wider, within the bound.
A program may use at most 64 MiB of HBM per device.

v0:
```python
import jax
import jax.numpy as jnp
from jax import lax
from jax.sharding import PartitionSpec as P

decay_rate = 0.99


def in_blocks(x, dim, size):
    shape = x.shape
    parts = x.reshape(*shape[:dim], size, shape[dim] // size, *shape[dim + 1 :])
    return jnp.moveaxis(parts, dim, 0)


def summed_on_arrival(x, axis, dim):
    size = lax.axis_size(axis)
    parts = lax.all_to_all(in_blocks(x, dim, size), axis, 0, 0, tiled=True)
    return jnp.sum(parts.astype(jnp.float32), axis=0)


def on_device(partial_grad, owner_table, left_stat, right_stat, left_root, right_root):
    local_grad = partial_grad[0]
    block_count = local_grad.shape[0]
    my_row = lax.dynamic_index_in_dim(owner_table, lax.axis_index("fsdp"), 0, keepdims=False)
    is_filled = my_row >= 0
    sender_index = jnp.maximum(owner_table.T, 0)
    sender_mask = owner_table.T >= 0
    shares = summed_on_arrival(
        local_grad.astype(jnp.float32).astype(jnp.bfloat16), "rep", 2
    ).astype(jnp.bfloat16)
    picked = jnp.take(shares, sender_index, axis=0)
    picked = jnp.where(sender_mask[:, :, None, None], picked, jnp.zeros((), picked.dtype))
    columns = lax.all_to_all(
        picked.reshape(picked.shape[0], -1, picked.shape[3]),
        "fsdp",
        split_axis=1,
        concat_axis=1,
        tiled=True,
    )
    gradient = lax.all_gather(columns, "rep", axis=2, tiled=True)
    share_width = left_stat.shape[3]
    first_col = lax.axis_index("rep") * share_width
    rows_share = lax.dynamic_slice_in_dim(gradient, first_col, share_width, 1)
    cols_share = lax.dynamic_slice_in_dim(gradient, first_col, share_width, 2)
    left_term = jnp.einsum("sik,sjk->sij", gradient, rows_share, preferred_element_type=jnp.float32)
    right_term = jnp.einsum(
        "ski,skj->sij", gradient, cols_share, preferred_element_type=jnp.float32
    )
    keeper = is_filled[:, None, None]
    left_next = jnp.where(
        keeper, decay_rate * left_stat[0] + (1.0 - decay_rate) * left_term, left_stat[0]
    )
    right_next = jnp.where(
        keeper, decay_rate * right_stat[0] + (1.0 - decay_rate) * right_term, right_stat[0]
    )
    applied = jnp.einsum(
        "sik,skj->sij",
        lax.all_gather(left_root[0], "rep", axis=2, tiled=True),
        gradient,
        preferred_element_type=jnp.float32,
    ).astype(jnp.bfloat16)
    result_cols = jnp.einsum(
        "sik,skj->sij", applied, right_root[0], preferred_element_type=jnp.float32
    ).astype(jnp.bfloat16)
    returned = lax.all_to_all(result_cols, "fsdp", split_axis=1, concat_axis=0, tiled=True)
    flat_table = owner_table.reshape(-1)
    slot_ids = jnp.arange(flat_table.shape[0], dtype=jnp.int32)
    block_ids = jnp.arange(block_count, dtype=jnp.int32)
    positions = jnp.sum(
        jnp.where(flat_table[None, :] == block_ids[:, None], slot_ids[None, :], 0), axis=1
    )
    update = jnp.take(returned, positions, axis=0)
    return (left_next[None], right_next[None], update)


def solution(mesh):
    return jax.shard_map(
        on_device,
        mesh=mesh,
        in_specs=(
            P("rep", None, "fsdp", None),
            P(),
            P("fsdp", None, None, "rep"),
            P("fsdp", None, None, "rep"),
            P("fsdp", None, None, "rep"),
            P("fsdp", None, None, "rep"),
        ),
        out_specs=(
            P("fsdp", None, None, "rep"),
            P("fsdp", None, None, "rep"),
            P(None, "fsdp", "rep"),
        ),
        check_vma=False,
    )
```

profile of v0, /device:TPU:1, one launch (start us, length us, event | category | flops | bytes accessed | tf_op | source)
XLA Modules:
  0.0 213.5 jit_solution(4872526677755833323)
XLA Ops:
  7.2 0.0 copy-start
  7.2 0.0 all-gather.6.cloned.1.call-start
  7.2 0.7 all-gather.6.cloned.1.call-update
  7.9 3.3 %reshape.46 = bf16[64,16,4,256]{3,2,1,0:T(4,128)(2,1)S(1)} reshape(bf16[1,64,16,1024]{3,2,1,0:T(8,128)(2,1)} %param.6) | data formatting | bytes 4194304 | tf_op jit(solution)/shard_map/reshape | solution.py:11
  11.3 1.6 copy.32
  12.9 0.0 copy-start.1
  12.9 5.0 %all-to-all-start = ((bf16[4,64,16,256]{3,2,1,0:T(8,128)(2,1)}), bf16[4,64,16,256]{3,2,1,0:T(8,128)(2,1)S(1)}, u32[]{:S(2)}, u32[]{:S(2)}) async-start(bf16[4,64,16,256]{3,2,1,0:T(8,128)(2,1)} %copy.32), calls=%async_computation | async-start | bytes 4194304 | tf_op jit(solution)/shard_map/all_to_all | solution.py:17
  17.8 0.0 all-gather.4.cloned.1.call-start
  17.8 0.0 copy-done.1
  17.8 0.1 reshape.49
  17.9 0.1 broadcast_in_dim.76
  18.0 0.1 broadcast_in_dim.77
  18.1 0.1 broadcast_in_dim.79
  18.2 0.1 broadcast_in_dim.80
  18.4 35.2 %all-to-all-done = bf16[4,64,16,256]{3,2,1,0:T(8,128)(2,1)S(1)} async-done(((bf16[4,64,16,256]{3,2,1,0:T(8,128)(2,1)}), bf16[4,64,16,256]{3,2,1,0:T(8,128)(2,1)S(1)}, u32[]{:S(2)}, u32[]{:S(2)}) %all-to-all-start) | async-done | bytes 2097184 | tf_op jit(solution)/shard_map/all_to_all | solution.py:17
  53.5 1.2 reduce_sum.23
  54.8 1.7 gather_fusion
  56.5 0.9 fusion.18
  57.4 1.1 copy.33
  58.5 42.5 %all_to_all.28 = bf16[2,1024,256]{2,0,1:T(2,128)(2,1)S(1)} all-to-all(bf16[2,1024,256]{2,0,1:T(2,128)(2,1)S(1)} %copy.33), channel_id=1, replica_groups=mesh['fsdp'=64,'rep'=4] {'fsdp'}, dimensions={1} | all-to-all | bytes 2097152 | tf_op jit(solution)/shard_map/all_to_all | solution.py:33
  101.0 1.1 copy.34
  102.2 0.0 all-gather.4.cloned.1.call-update
  102.2 0.0 all-gather.6.cloned.1.call-done
  102.2 50.5 %all-gather.4.cloned.1.call-done = bf16[2,1024,1024]{2,1,0:T(8,128)(2,1)} async-done(((bf16[2,1024,256]{2,1,0:T(8,128)(2,1)}), bf16[2,1024,1024]{2,1,0:T(8,128)(2,1)}) %all-gather.4.cloned.1.call-update) | async-done | bytes 4194320 | tf_op jit(solution)/shard_map/all_gather | solution.py:40
  152.7 0.0 copy-done
  152.7 9.9 %fusion.12 = bf16[2,1024,256]{2,1,0:T(8,128)(2,1)S(1)} fusion(bf16[2,1024,1024]{2,1,0:T(8,128)(2,1)} %all-gather.4.cloned.1.call-done, bf16[1,2,1024,1024]{3,2,1,0:T(8,128)(2,1)} %all-gather.6.cloned.1.call-done, bf16[1,2,1024,256]{3,2,1,0:T(8,128)(2,1)S(1)} %copy-done), kind=kOutput, calls=%fused_computation.14 | convolution fusion | flops 5371330560 | bytes 10485760 | tf_op jit(solution)/shard_map/sik,skj->sij/dot_general | solution.py:62
  162.5 2.1 copy.39
  164.6 12.1 %all-to-all-start.2 = ((bf16[2,1024,256]{2,0,1:T(2,128)(2,1)}), bf16[2,1024,256]{2,0,1:T(2,128)(2,1)S(1)}, u32[]{:S(2)}, u32[]{:S(2)}) async-start(bf16[2,1024,256]{2,0,1:T(2,128)(2,1)} %copy.39), calls=%async_computation.2 | async-start | bytes 2097152 | tf_op jit(solution)/shard_map/all_to_all | solution.py:65
  176.7 0.1 copy.36
  176.8 0.1 eq.15
  176.9 0.2 compare_reduce_fusion
  177.1 0.1 select_reduce_fusion
  177.2 0.0 copy-start.2
  177.3 0.0 copy-start.3
  177.3 6.4 %fusion.5 = f32[1,2,1024,256]{3,2,1,0:T(8,128)} fusion(f32[1,2,1024,256]{3,2,1,0:T(8,128)} %param.9, bf16[2,1024,1024]{2,1,0:T(8,128)(2,1)} %all-gather.4.cloned.1.call-done, s32[]{:T(128)S(6)} %select_n.55, pred[2]{0:T(512)(128)(4,1)S(1)} %compare_reduce_fusion), kind=kOutput, calls=%fused_computation.9 | convolution fusion | flops 1075838976 | bytes 9437190 | tf_op jit(solution)/shard_map/ski,skj->sij/dot_general | solution.py:46
  183.7 0.0 copy-done.2
  183.7 0.0 copy-done.3
  183.7 2.7 %fusion.7 = f32[1,2,1024,256]{3,2,1,0:T(8,128)} fusion(f32[1,2,1024,256]{3,2,1,0:T(8,128)S(1)} %copy-done.3, bf16[2,1024,1024]{2,1,0:T(8,128)(2,1)S(1)} %copy-done.2, s32[]{:T(128)S(6)} %select_n.55, pred[2]{0:T(512)(128)(4,1)S(1)} %compare_reduce_fusion), kind=kOutput, calls=%fused_computation.13 | convolution fusion | flops 1075838976 | bytes 9437700 | tf_op jit(solution)/shard_map/sik,sjk->sij/dot_general | solution.py:45
  186.5 18.4 %all-to-all-done.2 = bf16[2,1024,256]{2,0,1:T(2,128)(2,1)S(1)} async-done(((bf16[2,1024,256]{2,0,1:T(2,128)(2,1)}), bf16[2,1024,256]{2,0,1:T(2,128)(2,1)S(1)}, u32[]{:S(2)}, u32[]{:S(2)}) %all-to-all-start.2) | async-done | bytes 1048608 | tf_op jit(solution)/shard_map/all_to_all | solution.py:65
  204.8 0.1 copy.40
  205.0 0.1 copy.41
  205.1 0.6 gather_fusion.1
  205.7 0.9 broadcast_select_fusion
  (7 shorter events, 0.0 us)
Async XLA Ops:
  7.2 145.5 %copy-start = (bf16[1,2,1024,256]{3,2,1,0:T(8,128)(2,1)S(1)}, bf16[1,2,1024,256]{3,2,1,0:T(8,128)(2,1)}, u32[]{:S(2)}) copy-start(bf16[1,2,1024,256]{3,2,1,0:T(8,128)(2,1)} %param.11) | copy-start | bytes 3145732
  7.2 95.0 %all-gather.6.cloned.1.call-start = ((), (), s32[]{:S(2)}) async-start(), calls=%async_computation.4 | async-start | bytes 5242880 | tf_op jit(solution)/shard_map/all_gather | solution.py:58
  12.9 5.0 %copy-start.1 = (s32[64,2]{0,1:T(2,128)S(1)}, s32[64,2]{0,1:T(2,128)}, u32[]{:S(2)}) copy-start(s32[64,2]{0,1:T(2,128)} %param.7) | copy-start | bytes 1540
  12.9 40.7 %all-to-all-start = ((bf16[4,64,16,256]{3,2,1,0:T(8,128)(2,1)}), bf16[4,64,16,256]{3,2,1,0:T(8,128)(2,1)S(1)}, u32[]{:S(2)}, u32[]{:S(2)}) async-start(bf16[4,64,16,256]{3,2,1,0:T(8,128)(2,1)} %copy.32), calls=%async_computation | async-start | bytes 4194304 | tf_op jit(solution)/shard_map/all_to_all | solution.py:17
  17.8 134.8 %all-gather.4.cloned.1.call-start = ((), (), s32[]{:S(2)}) async-start(), calls=%async_computation.3 | async-start | bytes 5242880 | tf_op jit(solution)/shard_map/all_gather | solution.py:40
  164.6 40.2 %all-to-all-start.2 = ((bf16[2,1024,256]{2,0,1:T(2,128)(2,1)}), bf16[2,1024,256]{2,0,1:T(2,128)(2,1)S(1)}, u32[]{:S(2)}, u32[]{:S(2)}) async-start(bf16[2,1024,256]{2,0,1:T(2,128)(2,1)} %copy.39), calls=%async_computation.2 | async-start | bytes 2097152 | tf_op jit(solution)/shard_map/all_to_all | solution.py:65
  177.2 6.5 %copy-start.2 = (bf16[2,1024,1024]{2,1,0:T(8,128)(2,1)S(1)}, bf16[2,1024,1024]{2,1,0:T(8,128)(2,1)}, u32[]{:S(2)}) copy-start(bf16[2,1024,1024]{2,1,0:T(8,128)(2,1)} %all-gather.4.cloned.1.call-done) | copy-start | bytes 12582916
  177.3 6.5 %copy-start.3 = (f32[1,2,1024,256]{3,2,1,0:T(8,128)S(1)}, f32[1,2,1024,256]{3,2,1,0:T(8,128)}, u32[]{:S(2)}) copy-start(f32[1,2,1024,256]{3,2,1,0:T(8,128)} %param.8) | copy-start | bytes 6291460
Sparse Core Ops, SparseCore 0:
  9.8 70.3 all-gather.5
  102.3 50.3 all-gather.3
where the time goes:
time: 214 us
  waiting for transfers between devices  105 us (49%)
  blocking collectives  42.5 us (20%)
  matrix products  19 us (9%)
  starting transfers between devices  17.1 us (8%)
  between operations  14.2 us (7%)
  local copies, waits for them, and re-layouts  12.5 us (6%)
  other arithmetic  3.46 us (2%)
    all_gather x1, waiting for transfers between devices, on_device(): gradient = lax.all_gather(columns, 'rep', axis=2, tiled=True)  50.5 us
    all_to_all x1, blocking collectives, on_device(): lax.all_to_all(picked.reshape(picked.shape[0], -1, picked.shape[3]), 'fsd...  42.5 us
    all_to_all x1, waiting for transfers between devices, summed_on_arrival(): parts = lax.all_to_all(in_blocks(x, dim, size), axis, 0, 0, tiled=True)  35.2 us
    all_to_all x1, waiting for transfers between devices, on_device(): lax.all_to_all(result_cols, 'fsdp', split_axis=1, concat_axis=0, tiled=True)  18.4 us
    all_to_all x1, starting transfers between devices, on_device(): lax.all_to_all(result_cols, 'fsdp', split_axis=1, concat_axis=0, tiled=True)  12.1 us
    dot_general x1, matrix products, on_device(): jnp.einsum('sik,skj->sij', applied, right_root[0], preferred_element_type...  9.85 us
    dot_general x1, matrix products, on_device(): jnp.einsum('ski,skj->sij', gradient, cols_share, preferred_element_type=j...  6.45 us
    all_to_all x1, starting transfers between devices, summed_on_arrival(): parts = lax.all_to_all(in_blocks(x, dim, size), axis, 0, 0, tiled=True)  4.96 us
  transfers between devices with their start and end apart: 4, of which 3 were waited for; matrix products, arithmetic and copies ran while one was open for 10% of the time, Pallas kernels for 0%

commit v1 on v0

--- a/solution.py
+++ b/solution.py
@@ -37,7 +37,7 @@
         concat_axis=1,
         tiled=True,
     )
-    gradient = lax.all_gather(columns, "rep", axis=2, tiled=True)
+    gradient = jnp.concatenate(jax.lax.all_gather(columns, axis_name="rep"), axis=2)
     share_width = left_stat.shape[3]
     first_col = lax.axis_index("rep") * share_width
     rows_share = lax.dynamic_slice_in_dim(gradient, first_col, share_width, 1)

time: 214 us -> 252 us (1.18)
  waiting for transfers between devices: 105 us -> 138 us
  local copies, waits for them, and re-layouts: 12.5 us -> 17.3 us
    all_gather x1, waiting for transfers between devices: 0.02 us -> 50.2 us  [on_device(): lax.all_gather(left_root[0], 'rep', axis=2, tiled=True)]
    all_to_all x1, waiting for transfers between devices: 35.2 us -> 24 us  [summed_on_arrival(): parts = lax.all_to_all(in_blocks(x, dim, size), axis, 0, 0, tiled=True)]
    all_gather x1, waiting for transfers between devices: 50.5 us -> 45 us  [on_device(): jax.lax.all_gather(columns, axis_name='rep')]
    reshape x0 -> x1, local copies, waits for them, and re-layouts: none -> 4.71 us  [on_device(): jnp.concatenate(jax.lax.all_gather(columns, axis_name='rep'), axis=2)]
  transfers between devices with their start and end apart: 4 -> 4, of which waited for: 3 -> 4; matrix products, arithmetic and copies ran while one was open for 10% -> 6% of each run, Pallas kernels for 0% -> 0%
where the time goes in v1:
time: 252 us
  waiting for transfers between devices  138 us (55%)
  blocking collectives  42.4 us (17%)
  matrix products  19.1 us (8%)
  local copies, waits for them, and re-layouts  17.3 us (7%)
  starting transfers between devices  17.1 us (7%)
  between operations  14.2 us (6%)
  other arithmetic  3.45 us (1%)
    all_gather x1, waiting for transfers between devices, on_device(): lax.all_gather(left_root[0], 'rep', axis=2, tiled=True)  50.2 us
    all_gather x1, waiting for transfers between devices, on_device(): jax.lax.all_gather(columns, axis_name='rep')  45 us
    all_to_all x1, blocking collectives, on_device(): lax.all_to_all(picked.reshape(picked.shape[0], -1, picked.shape[3]), 'fsd...  42.4 us
    all_to_all x1, waiting for transfers between devices, summed_on_arrival(): parts = lax.all_to_all(in_blocks(x, dim, size), axis, 0, 0, tiled=True)  24 us
    all_to_all x1, waiting for transfers between devices, on_device(): lax.all_to_all(result_cols, 'fsdp', split_axis=1, concat_axis=0, tiled=True)  18.3 us
    all_to_all x1, starting transfers between devices, on_device(): lax.all_to_all(result_cols, 'fsdp', split_axis=1, concat_axis=0, tiled=True)  12.1 us
    dot_general x1, matrix products, on_device(): jnp.einsum('sik,skj->sij', applied, right_root[0], preferred_element_type...  9.85 us
    dot_general x1, matrix products, on_device(): jnp.einsum('ski,skj->sij', gradient, cols_share, preferred_element_type=j...  6.45 us
  transfers between devices with their start and end apart: 4, of which 4 were waited for; matrix products, arithmetic and copies ran while one was open for 6% of the time, Pallas kernels for 0%

profile of v1, /device:TPU:1, one launch (start us, length us, event | category | flops | bytes accessed | tf_op | source)
XLA Modules:
  0.0 251.7 jit_solution(9658902887312768706)
XLA Ops:
  7.2 0.0 copy-start
  7.2 3.4 %reshape.52 = bf16[64,16,4,256]{3,2,1,0:T(4,128)(2,1)S(1)} reshape(bf16[1,64,16,1024]{3,2,1,0:T(8,128)(2,1)} %param.6) | data formatting | bytes 4194304 | tf_op jit(solution)/shard_map/reshape | solution.py:11
  10.6 1.6 copy.35
  12.2 0.0 copy-start.2
  12.2 5.0 %all-to-all-start = ((bf16[4,64,16,256]{3,2,1,0:T(8,128)(2,1)}), bf16[4,64,16,256]{3,2,1,0:T(8,128)(2,1)S(1)}, u32[]{:S(2)}, u32[]{:S(2)}) async-start(bf16[4,64,16,256]{3,2,1,0:T(8,128)(2,1)} %copy.35), calls=%async_computation | async-start | bytes 4194304 | tf_op jit(solution)/shard_map/all_to_all | solution.py:17
  17.2 0.0 all-gather.5.cloned.1.call-start
  17.2 0.0 copy-done.2
  17.2 0.1 reshape.57
  17.3 0.1 broadcast_in_dim.76
  17.4 0.1 broadcast_in_dim.77
  17.5 0.1 broadcast_in_dim.79
  17.6 0.1 broadcast_in_dim.80
  17.7 24.0 %all-to-all-done = bf16[4,64,16,256]{3,2,1,0:T(8,128)(2,1)S(1)} async-done(((bf16[4,64,16,256]{3,2,1,0:T(8,128)(2,1)}), bf16[4,64,16,256]{3,2,1,0:T(8,128)(2,1)S(1)}, u32[]{:S(2)}, u32[]{:S(2)}) %all-to-all-start) | async-done | bytes 2097184 | tf_op jit(solution)/shard_map/all_to_all | solution.py:17
  41.7 1.2 reduce_sum.23
  42.9 1.7 gather_fusion
  44.6 0.9 fusion.18
  45.5 1.1 copy.36
  46.6 42.4 %all_to_all.28 = bf16[2,1024,256]{2,0,1:T(2,128)(2,1)S(1)} all-to-all(bf16[2,1024,256]{2,0,1:T(2,128)(2,1)S(1)} %copy.36), channel_id=1, replica_groups=mesh['fsdp'=64,'rep'=4] {'fsdp'}, dimensions={1} | all-to-all | bytes 2097152 | tf_op jit(solution)/shard_map/all_to_all | solution.py:33
  89.1 1.1 copy.37
  90.2 0.0 all-gather.5.cloned.1.call-update
  90.2 0.0 all-gather.7.cloned.1.call-start
  90.2 0.7 all-gather.7.cloned.1.call-update
  90.9 45.0 %all-gather.5.cloned.1.call-done = bf16[8,1024,256]{2,1,0:T(8,128)(2,1)} async-done(((bf16[2,1024,256]{2,1,0:T(8,128)(2,1)}), bf16[8,1024,256]{2,1,0:T(8,128)(2,1)}) %all-gather.5.cloned.1.call-update) | async-done | bytes 4194320 | tf_op jit(solution)/shard_map/all_gather | solution.py:40
  136.0 4.7 %copy.49 = bf16[4,2,128,8,256]{4,3,0,2,1:T(8,128)(2,1)} copy(bf16[4,2,128,8,256]{4,3,2,1,0:T(8,128)(2,1)} %bitcast.68) | data formatting | bytes 8388608 | tf_op jit(solution)/shard_map/reshape | solution.py:40
  140.7 50.2 %all-gather.7.cloned.1.call-done = bf16[1,2,1024,1024]{3,2,1,0:T(8,128)(2,1)} async-done(((bf16[1,2,1024,256]{3,2,1,0:T(8,128)(2,1)}), bf16[1,2,1024,1024]{3,2,1,0:T(8,128)(2,1)}) %all-gather.7.cloned.1.call-update) | async-done | bytes 4194320 | tf_op jit(solution)/shard_map/all_gather | solution.py:58
  190.9 0.0 copy-done
  190.9 9.9 %fusion.12 = bf16[2,1024,256]{2,1,0:T(8,128)(2,1)S(1)} fusion(bf16[2,1024,1024]{2,1,0:T(8,128)(2,1)} %bitcast.65, bf16[1,2,1024,1024]{3,2,1,0:T(8,128)(2,1)} %all-gather.7.cloned.1.call-done, bf16[1,2,1024,256]{3,2,1,0:T(8,128)(2,1)S(1)} %copy-done), kind=kOutput, calls=%fused_computation.14 | convolution fusion | flops 5371330560 | bytes 10485760 | tf_op jit(solution)/shard_map/sik,skj->sij/dot_general | solution.py:62
  200.7 2.1 copy.43
  202.8 12.1 %all-to-all-start.2 = ((bf16[2,1024,256]{2,0,1:T(2,128)(2,1)}), bf16[2,1024,256]{2,0,1:T(2,128)(2,1)S(1)}, u32[]{:S(2)}, u32[]{:S(2)}) async-start(bf16[2,1024,256]{2,0,1:T(2,128)(2,1)} %copy.43), calls=%async_computation.2 | async-start | bytes 2097152 | tf_op jit(solution)/shard_map/all_to_all | solution.py:65
  214.9 0.1 copy.40
  215.0 0.1 eq.15
  215.1 0.2 compare_reduce_fusion
  215.3 0.1 select_reduce_fusion
  215.4 0.0 copy-start.1
  215.5 0.0 copy-start.3
  215.5 6.4 %fusion.5 = f32[1,2,1024,256]{3,2,1,0:T(8,128)} fusion(f32[1,2,1024,256]{3,2,1,0:T(8,128)} %param.9, bf16[2,1024,1024]{2,1,0:T(8,128)(2,1)} %bitcast.66, s32[]{:T(128)S(6)} %select_n.55, pred[2]{0:T(512)(128)(4,1)S(1)} %compare_reduce_fusion), kind=kOutput, calls=%fused_computation.9 | convolution fusion | flops 1075838976 | bytes 9437190 | tf_op jit(solution)/shard_map/ski,skj->sij/dot_general | solution.py:46
  221.9 0.0 copy-done.1
  221.9 0.0 copy-done.3
  221.9 2.8 %fusion.7 = f32[1,2,1024,256]{3,2,1,0:T(8,128)} fusion(f32[1,2,1024,256]{3,2,1,0:T(8,128)S(1)} %copy-done.3, bf16[2,1024,1024]{2,1,0:T(8,128)(2,1)S(1)} %bitcast.67, s32[]{:T(128)S(6)} %select_n.55, pred[2]{0:T(512)(128)(4,1)S(1)} %compare_reduce_fusion), kind=kOutput, calls=%fused_computation.13 | convolution fusion | flops 1075838976 | bytes 9437700 | tf_op jit(solution)/shard_map/sik,sjk->sij/dot_general | solution.py:45
  224.7 18.3 %all-to-all-done.2 = bf16[2,1024,256]{2,0,1:T(2,128)(2,1)S(1)} async-done(((bf16[2,1024,256]{2,0,1:T(2,128)(2,1)}), bf16[2,1024,256]{2,0,1:T(2,128)(2,1)S(1)}, u32[]{:S(2)}, u32[]{:S(2)}) %all-to-all-start.2) | async-done | bytes 1048608 | tf_op jit(solution)/shard_map/all_to_all | solution.py:65
  243.0 0.1 copy.44
  243.2 0.1 copy.45
  243.3 0.6 gather_fusion.1
  243.9 0.9 broadcast_select_fusion
  (7 shorter events, 0.0 us)
Async XLA Ops:
  7.2 183.7 %copy-start = (bf16[1,2,1024,256]{3,2,1,0:T(8,128)(2,1)S(1)}, bf16[1,2,1024,256]{3,2,1,0:T(8,128)(2,1)}, u32[]{:S(2)}) copy-start(bf16[1,2,1024,256]{3,2,1,0:T(8,128)(2,1)} %param.11) | copy-start | bytes 3145732
  12.2 5.0 %copy-start.2 = (s32[64,2]{0,1:T(2,128)S(1)}, s32[64,2]{0,1:T(2,128)}, u32[]{:S(2)}) copy-start(s32[64,2]{0,1:T(2,128)} %param.7) | copy-start | bytes 1540
  12.2 29.4 %all-to-all-start = ((bf16[4,64,16,256]{3,2,1,0:T(8,128)(2,1)}), bf16[4,64,16,256]{3,2,1,0:T(8,128)(2,1)S(1)}, u32[]{:S(2)}, u32[]{:S(2)}) async-start(bf16[4,64,16,256]{3,2,1,0:T(8,128)(2,1)} %copy.35), calls=%async_computation | async-start | bytes 4194304 | tf_op jit(solution)/shard_map/all_to_all | solution.py:17
  17.2 118.8 %all-gather.5.cloned.1.call-start = ((), (), s32[]{:S(2)}) async-start(), calls=%async_computation.3 | async-start | bytes 5242880 | tf_op jit(solution)/shard_map/all_gather | solution.py:40
  90.2 100.7 %all-gather.7.cloned.1.call-start = ((), (), s32[]{:S(2)}) async-start(), calls=%async_computation.4 | async-start | bytes 5242880 | tf_op jit(solution)/shard_map/all_gather | solution.py:58
  202.8 40.2 %all-to-all-start.2 = ((bf16[2,1024,256]{2,0,1:T(2,128)(2,1)}), bf16[2,1024,256]{2,0,1:T(2,128)(2,1)S(1)}, u32[]{:S(2)}, u32[]{:S(2)}) async-start(bf16[2,1024,256]{2,0,1:T(2,128)(2,1)} %copy.43), calls=%async_computation.2 | async-start | bytes 2097152 | tf_op jit(solution)/shard_map/all_to_all | solution.py:65
  215.4 6.5 %copy-start.1 = (bf16[4,2,128,8,256]{4,3,0,2,1:T(8,128)(2,1)S(1)}, bf16[4,2,128,8,256]{4,3,0,2,1:T(8,128)(2,1)}, u32[]{:S(2)}) copy-start(bf16[4,2,128,8,256]{4,3,0,2,1:T(8,128)(2,1)} %copy.49) | copy-start | bytes 12582916
  215.5 6.5 %copy-start.3 = (f32[1,2,1024,256]{3,2,1,0:T(8,128)S(1)}, f32[1,2,1024,256]{3,2,1,0:T(8,128)}, u32[]{:S(2)}) copy-start(f32[1,2,1024,256]{3,2,1,0:T(8,128)} %param.8) | copy-start | bytes 6291460
Sparse Core Ops, SparseCore 0:
  90.3 45.6 all-gather.4
  137.8 53.0 all-gather.6
